TPU v7x, 16 devices: a whole 2x2x2 slice. The times are simulated.
16 devices in a mesh: dp: 2 (over z), ep: 8 (over y, x, core).
Axes of the slice: x: 2, y: 2, z: 2, core: 2. Of those that a mesh axis runs over, the one named last changes fastest.
Arguments:
- x_tokens: bfloat16 [131072, 768], P(('dp', 'ep'))
- modality: int32 [131072], P(('dp', 'ep'))
- router: float32 [768, 32], replicated
- expert_ids: int32 [131072], P(('dp', 'ep'))
- priority: int32 [131072], P(('dp', 'ep'))
- w_in: bfloat16 [32, 768, 3072], P('ep')
- b_in: bfloat16 [32, 3072], P('ep')
- w_out: bfloat16 [32, 3072, 768], P('ep')
- b_out: bfloat16 [32, 768], P('ep')
- dy_out: bfloat16 [131072, 768], P(('dp', 'ep'))
Outputs:
- output 1: bfloat16 [131072, 768], P(('dp', 'ep'))
- output 2: float32 [], replicated
- output 3: bfloat16 [131072, 768], P(('dp', 'ep'))
- output 4: float32 [768, 32], replicated
- output 5: bfloat16 [32, 768, 3072], P('ep')
- output 6: bfloat16 [32, 3072], P('ep')
- output 7: bfloat16 [32, 3072, 768], P('ep')
- output 8: bfloat16 [32, 768], P('ep')
All inputs are finite; a program needn't handle non-finite values.
Results may differ from a plain program's by a relative error of at most 0.00946785.
Values are sent between devices in bfloat16 or wider.
A program may use at most 1 GiB of HBM per device.

v0:
```python
import jax
import jax.numpy as jnp
from jax import lax
from jax.sharding import PartitionSpec as P

ALL_AXES = ("dp", "ep")


def route_tokens(expert_ids, priority, num_experts, capacity):
    num_tokens = expert_ids.shape[0]
    sort_order = jnp.argsort(expert_ids * num_tokens + priority)
    sorted_rank = jnp.argsort(sort_order)
    counts = jnp.sum((expert_ids[:, None] == jnp.arange(num_experts)[None, :]).astype(jnp.int32), axis=0)
    starts = jnp.cumsum(counts) - counts
    slot_rank = jnp.arange(capacity)
    slot_token = sort_order[jnp.minimum(starts[:, None] + slot_rank[None, :], num_tokens - 1)]
    slot_valid = slot_rank[None, :] < counts[:, None]
    position = sorted_rank - starts[expert_ids]
    keep_mask = position < capacity
    token_slot = expert_ids * capacity + jnp.minimum(position, capacity - 1)
    return slot_token, slot_valid, token_slot, keep_mask


def router_forward(x_loc, modality, router, expert_ids):
    num_experts = router.shape[1]
    logits = jnp.dot(x_loc, router, precision=lax.Precision.HIGHEST, preferred_element_type=jnp.float32)
    log_probs = jax.nn.log_softmax(logits, axis=-1)
    router_probs = jnp.exp(log_probs)
    expert_onehot = (expert_ids[:, None] == jnp.arange(num_experts)[None, :]).astype(jnp.float32)
    gate_prob = jnp.sum(router_probs * expert_onehot, axis=-1)
    mod_mask = jnp.stack([modality == 0, modality == 1]).astype(jnp.float32)
    entropy = -jnp.sum(router_probs * log_probs, axis=-1)
    local_stats = jnp.concatenate([jnp.dot(mod_mask, router_probs), jnp.dot(mod_mask, entropy)[:, None], jnp.sum(mod_mask, axis=1, keepdims=True)], axis=1)
    return log_probs, router_probs, expert_onehot, gate_prob, mod_mask, local_stats


def aux_from_stats(stats, num_experts):
    mod_count = stats[:, num_experts + 1]
    mean_probs = stats[:, :num_experts] / mod_count[:, None]
    aux_loss = jnp.sum(stats[:, num_experts] / mod_count) + jnp.sum(mean_probs * jnp.log(mean_probs))
    return aux_loss, mean_probs, mod_count


def router_backward(x_loc, router, log_probs, router_probs, expert_onehot, mod_mask, mean_probs, mod_count, d_gate):
    inv_count = jnp.dot(1.0 / mod_count, mod_mask)
    global_part = jnp.einsum("mt,me->te", mod_mask, jnp.log(mean_probs) / mod_count[:, None])
    d_probs = expert_onehot * d_gate[:, None] + global_part - log_probs * inv_count[:, None]
    d_logits = router_probs * (d_probs - jnp.sum(d_probs * router_probs, axis=-1, keepdims=True))
    d_router_part = jnp.einsum("tw,te->we", x_loc, d_logits, precision=lax.Precision.HIGHEST, preferred_element_type=jnp.float32)
    dx_router = jnp.einsum("te,we->tw", d_logits, router, precision=lax.Precision.HIGHEST, preferred_element_type=jnp.float32)
    return d_router_part, dx_router.astype(jnp.bfloat16)


def solution(mesh):
    token_spec = P(ALL_AXES)
    expert_spec = P("ep")

    def local_step(x_loc, modality, router, expert_ids, priority, w_in, b_in, w_out, b_out, dy_loc):
        num_tokens, model_width = x_loc.shape
        num_experts = router.shape[1]
        capacity = num_tokens // num_experts
        slot_token, slot_valid, token_slot, keep_mask = route_tokens(expert_ids, priority, num_experts, capacity)
        log_probs, router_probs, expert_onehot, gate_prob, mod_mask, local_stats = router_forward(x_loc, modality, router, expert_ids)
        aux_loss, mean_probs, mod_count = aux_from_stats(lax.psum(local_stats, ALL_AXES), num_experts)
        keep_col = keep_mask[:, None]
        slot_col = slot_valid[:, :, None]
        send_rows = jnp.where(slot_col, x_loc[slot_token], 0).astype(jnp.bfloat16)
        recv_rows = lax.all_to_all(send_rows, "ep", 0, 1, tiled=True)
        act_in = jnp.einsum("ecw,ewf->ecf", recv_rows, w_in, preferred_element_type=jnp.float32) + b_in[:, None, :].astype(jnp.float32)
        act_out, gelu_pullback = jax.vjp(jax.nn.gelu, act_in)
        hidden = act_out.astype(jnp.bfloat16)
        expert_out = jnp.einsum("ecf,efw->ecw", hidden, w_out, preferred_element_type=jnp.float32) + b_out[:, None, :].astype(jnp.float32)
        back_rows = lax.all_to_all(expert_out.astype(jnp.bfloat16), "ep", 1, 0, tiled=True)
        y_tok = back_rows.reshape(num_experts * capacity, model_width)[token_slot].astype(jnp.float32)
        out_tokens = jnp.where(keep_col, gate_prob[:, None] * y_tok, 0.0).astype(jnp.bfloat16)
        dy_f32 = dy_loc.astype(jnp.float32)
        d_gate = jnp.where(keep_mask, jnp.sum(dy_f32 * y_tok, axis=-1), 0.0)
        d_ytok = jnp.where(keep_col, gate_prob[:, None] * dy_f32, 0.0).astype(jnp.bfloat16)
        d_send = jnp.where(slot_col, d_ytok[slot_token], 0).astype(jnp.bfloat16)
        d_recv = lax.all_to_all(d_send, "ep", 0, 1, tiled=True)
        d_b_out = jnp.sum(d_recv.astype(jnp.float32), axis=1)
        d_w_out = jnp.einsum("ecf,ecw->efw", hidden, d_recv, preferred_element_type=jnp.float32)
        d_hidden = jnp.einsum("ecw,efw->ecf", d_recv, w_out, preferred_element_type=jnp.float32).astype(jnp.bfloat16)
        d_act = gelu_pullback(d_hidden.astype(jnp.float32))[0]
        d_b_in = jnp.sum(d_act, axis=1)
        d_act_bf = d_act.astype(jnp.bfloat16)
        d_w_in = jnp.einsum("ecw,ecf->ewf", recv_rows, d_act_bf, preferred_element_type=jnp.float32)
        d_rows = jnp.einsum("ecf,ewf->ecw", d_act_bf, w_in, preferred_element_type=jnp.float32).astype(jnp.bfloat16)
        d_back = lax.all_to_all(d_rows, "ep", 1, 0, tiled=True)
        dx_expert = jnp.where(keep_col, d_back.reshape(num_experts * capacity, model_width)[token_slot], 0).astype(jnp.bfloat16)
        d_router_part, dx_router = router_backward(x_loc, router, log_probs, router_probs, expert_onehot, mod_mask, mean_probs, mod_count, d_gate)
        d_router = lax.psum(d_router_part, ALL_AXES)
        expert_grads = lax.psum((d_w_in, d_b_in, d_w_out, d_b_out), "dp")
        return (out_tokens, aux_loss, dx_expert + dx_router, d_router) + tuple(grad_sum.astype(jnp.bfloat16) for grad_sum in expert_grads)

    return jax.shard_map(
        local_step,
        mesh=mesh,
        in_specs=(token_spec, token_spec, P(), token_spec, token_spec, expert_spec, expert_spec, expert_spec, expert_spec, token_spec),
        out_specs=(token_spec, P(), token_spec, P(), expert_spec, expert_spec, expert_spec, expert_spec),
        check_vma=False,
    )
```

profile of v0, /device:TPU:0, one launch (start us, length us, event | category | flops | bytes accessed | tf_op | source)
XLA Modules:
  0.0 2983.8 jit_solution(2961824697887954936)
XLA Ops:
  16.2 45.5 %gather_fusion = s32[8192]{0:T(1024)S(1)} fusion(s32[8192]{0:T(1024)S(1)} %get-tuple-element.10, s32[8192]{0:T(1024)S(1)} %broadcast_clamp_fusion), kind=kCustom, calls=%fused_computation | custom fusion | bytes 98304 | tf_op jit(solution)/shard_map/gather | solution.py:16
  61.9 43.2 %gather_fusion.1 = bf16[8192,768]{1,0:T(8,128)(2,1)} fusion(bf16[8192,768]{1,0:T(8,128)(2,1)} %param.10, s32[8192]{0:T(1024)S(1)} %broadcast_clamp_fusion.1), kind=kCustom, calls=%fused_computation.1 | custom fusion | bytes 25198592 | tf_op jit(solution)/shard_map/gather | solution.py:67
  105.1 10.8 broadcast_select_fusion.1
  121.8 139.7 %all-to-all-done = bf16[32,256,768]{2,1,0:T(8,128)(2,1)} async-done(((bf16[32,256,768]{2,1,0:T(8,128)(2,1)}), bf16[32,256,768]{2,1,0:T(8,128)(2,1)}, u32[]{:S(2)}, u32[]{:S(2)}) %all-to-all-start) | async-done | bytes 12582944 | tf_op jit(solution)/shard_map/all_to_all | solution.py:68
  272.2 74.6 %multiply_convert_fusion = (bf16[4,2048,3072]{2,1,0:T(8,128)(2,1)}, f32[4,2048,3072]{2,1,0:T(8,128)}) fusion(f32[4,3072]{1,0:T(4,128)S(1)} %convert_element_type.70, bf16[4,2048,768]{2,1,0:T(8,128)(2,1)} %bitcast.96, bf16[4,768,3072]{2,1,0:T(8,128)(2,1)} %param.15), kind=kOutput, calls=%fused_computation.18 | convolution fusion | flops 38906363904 | bytes 182501376 | tf_op jit(solution)/shard_map/ecw,ewf->ecf/dot_general | solution.py:69
  346.8 48.2 %add_convert_fusion = bf16[4,2048,768]{2,1,0:T(8,128)(2,1)} fusion(f32[4,768]{1,0:T(4,128)S(1)} %convert_element_type.72, bf16[4,2048,3072]{2,1,0:T(8,128)(2,1)} %get-tuple-element.64, bf16[4,3072,768]{2,1,0:T(8,128)(2,1)} %param.17), kind=kOutput, calls=%fused_computation.32 | convolution fusion | flops 38667288576 | bytes 81801216 | tf_op jit(solution)/shard_map/ecf,efw->ecw/dot_general | solution.py:72
  394.9 17.2 copy.47
  424.9 13.8 fusion.37
  440.2 142.4 %psum.42 = f32[2,34]{1,0:T(2,128)S(1)} all-reduce(f32[2,34]{1,0:T(2,128)S(1)} %pad_maximum_fusion), channel_id=1, replica_groups=mesh['dp'=2,'ep'=8] {'dp','ep'}, use_global_device_ids=true, to_apply=%region_9.10 | all-reduce | flops 68 | bytes 544 | tf_op jit(solution)/shard_map/psum | solution.py:64
  584.4 20.2 fusion.29
  604.6 11.7 copy.48
  616.3 43.2 %gather_fusion.2 = bf16[8192,768]{1,0:T(8,128)(2,1)} fusion(bf16[8192,768]{1,0:T(8,128)(2,1)} %bitcast.93, s32[8192]{0:T(1024)S(1)} %get-tuple-element.24), kind=kCustom, calls=%fused_computation.2 | custom fusion | bytes 25198592 | tf_op jit(solution)/shard_map/gather | solution.py:74
  671.6 15.7 fusion.12
  687.3 43.2 %gather_fusion.3 = bf16[8192,768]{1,0:T(8,128)(2,1)} fusion(bf16[8192,768]{1,0:T(8,128)(2,1)} %get-tuple-element.26, s32[8192]{0:T(1024)S(1)} %copy-done.16), kind=kCustom, calls=%fused_computation.3 | custom fusion | bytes 25198592 | tf_op jit(solution)/shard_map/gather | solution.py:79
  759.1 127.4 %all-to-all-done.2 = bf16[32,256,768]{2,1,0:T(8,128)(2,1)} async-done(((bf16[32,256,768]{2,1,0:T(8,128)(2,1)}), bf16[32,256,768]{2,1,0:T(8,128)(2,1)}, u32[]{:S(2)}, u32[]{:S(2)}) %all-to-all-start.2) | async-done | bytes 12582944 | tf_op jit(solution)/shard_map/all_to_all | solution.py:80
  904.1 51.0 %fusion.39 = f32[4,3072,768]{2,1,0:T(8,128)} fusion(bf16[4,2048,3072]{2,1,0:T(8,128)(2,1)} %get-tuple-element.64, bf16[4,2048,768]{2,1,0:T(8,128)(2,1)} %bitcast.98), kind=kOutput, calls=%fused_computation.90 | convolution fusion | flops 38654705664 | bytes 100663296 | tf_op jit(solution)/shard_map/ecf,ecw->efw/dot_general | solution.py:82
  955.1 114.1 %fusion.38 = (f32[4,3072]{1,0:T(4,128)}, bf16[4,2048,3072]{2,1,0:T(8,128)(2,1)}) fusion(f32[4,2048,3072]{2,1,0:T(8,128)} %get-tuple-element.65, f32[4,3072]{1,0:T(4,128)S(1)} %copy-done.24, bf16[4,2048,768]{2,1,0:T(8,128)(2,1)} %bitcast.99, bf16[4,3072,768]{2,1,0:T(8,128)(2,1)} %param.17), kind=kOutput, calls=%fused_computation.89 | convolution fusion | flops 39258673152 | bytes 182550528 | tf_op jit(solution)/shard_map/ecw,efw->ecf/dot_general | solution.py:83
  1069.2 49.5 %fusion.14 = f32[4,768,3072]{2,1,0:T(8,128)} fusion(bf16[4,2048,768]{2,1,0:T(8,128)(2,1)} %bitcast.97, bf16[4,2048,3072]{2,1,0:T(8,128)(2,1)} %get-tuple-element.68), kind=kOutput, calls=%fused_computation.28 | convolution fusion | flops 38654705664 | bytes 100663296 | tf_op jit(solution)/shard_map/ecw,ecf->ewf/dot_general | solution.py:87
  1118.7 48.3 %fusion.19 = bf16[4,2048,768]{2,1,0:T(8,128)(2,1)} fusion(bf16[4,768,3072]{2,1,0:T(8,128)(2,1)} %param.15, bf16[4,2048,3072]{2,1,0:T(8,128)(2,1)} %get-tuple-element.68), kind=kOutput, calls=%fused_computation.39 | convolution fusion | flops 38660997120 | bytes 81788928 | tf_op jit(solution)/shard_map/ecf,ewf->ecw/dot_general | solution.py:88
  1167.0 17.2 copy.52
  1189.7 1703.7 %all-reduce.5 = (bf16[4,768,3072]{2,1,0:T(8,128)(2,1)}, bf16[4,3072]{1,0:T(4,128)(2,1)}, bf16[4,3072,768]{2,1,0:T(8,128)(2,1)}, bf16[4,768]{1,0:T(4,128)(2,1)}) all-reduce(f32[4,768,3072]{2,1,0:T(8,128)} %fusion.14, f32[4,3072]{1,0:T(4,128)S(1)} %copy-done.25, f32[4,3072,768]{2,1,0:T(8,128)} %fusion.39, ...), channel_id=1, replica_groups=mesh['dp'=2,'ep'=8] {'dp'}, use_global_device_ids=true, to_apply=%region_15.16 | all-reduce | flops 18889728 | bytes 113338368 | tf_op jit(solution)/shard_map/psum | solution.py:93
  2893.5 11.7 copy.53
  2905.2 43.5 %gather_fusion.4 = bf16[8192,768]{1,0:T(8,128)(2,1)} fusion(bf16[8192,768]{1,0:T(8,128)(2,1)} %bitcast.92, s32[8192]{0:T(1024)S(1)} %copy-done.18), kind=kCustom, calls=%fused_computation.4 | custom fusion | bytes 25198592 | tf_op jit(solution)/shard_map/gather | solution.py:90
  2948.7 25.1 select_add_fusion
  (120 shorter events, 105.5 us)
Async XLA Ops:
  7.2 417.7 %copy-start = (f32[768,32]{0,1:T(8,128)S(1)}, f32[768,32]{0,1:T(8,128)}, u32[]{:S(2)}) copy-start(f32[768,32]{0,1:T(8,128)} %param.12) | copy-start | bytes 294916
  8.3 96.9 %copy-start.21 = (pred[32,256]{1,0:T(8,128)(4,1)}, pred[32,256]{1,0:T(8,128)(4,1)S(1)}, u32[]{:S(2)}) copy-start(pred[32,256]{1,0:T(8,128)(4,1)S(1)} %iota_compare_fusion.1) | copy-start | bytes 24580
  16.2 88.9 %copy-start.1 = (s32[8192]{0:T(1024)}, s32[8192]{0:T(1024)S(1)}, u32[]{:S(2)}) copy-start(s32[8192]{0:T(1024)S(1)} %get-tuple-element.10) | copy-start | bytes 98308
  115.9 145.6 %all-to-all-start = ((bf16[32,256,768]{2,1,0:T(8,128)(2,1)}), bf16[32,256,768]{2,1,0:T(8,128)(2,1)}, u32[]{:S(2)}, u32[]{:S(2)}) async-start(bf16[32,256,768]{2,1,0:T(8,128)(2,1)} %broadcast_select_fusion.1), calls=%async_computation | async-start | bytes 25165824 | tf_op jit(solution)/shard_map/all_to_all | solution.py:68
  121.8 225.0 %copy-start.23 = (f32[4,3072]{1,0:T(4,128)}, f32[4,3072]{1,0:T(4,128)S(1)}, u32[]{:S(2)}) copy-start(f32[4,3072]{1,0:T(4,128)S(1)} %convert_element_type.70) | copy-start | bytes 147460
  412.1 170.6 %copy-start.11 = (s32[32]{0:T(128)S(1)}, s32[32]{0:T(128)}, u32[]{:S(2)}) copy-start(s32[32]{0:T(128)} %copy-done.10) | copy-start | bytes 388
  412.1 172.3 %copy-start.14 = (s32[8192]{0:T(1024)S(1)}, s32[8192]{0:T(1024)}, u32[]{:S(2)}) copy-start(s32[8192]{0:T(1024)} %param.13) | copy-start | bytes 98308
  412.1 192.5 %all-to-all-start.1 = ((bf16[4,2048,768]{2,0,1:T(4,128)(2,1)}), bf16[4,2048,768]{2,0,1:T(4,128)(2,1)}, u32[]{:S(2)}, u32[]{:S(2)}) async-start(bf16[4,2048,768]{2,0,1:T(4,128)(2,1)} %copy.47), calls=%async_computation.1 | async-start | bytes 25165824 | tf_op jit(solution)/shard_map/all_to_all | solution.py:73
  438.6 310.6 %copy-start.4 = (f32[8192,32]{0,1:T(8,128)}, f32[8192,32]{0,1:T(8,128)S(1)}, u32[]{:S(2)}) copy-start(f32[8192,32]{0,1:T(8,128)S(1)} %get-tuple-element.63) | copy-start | bytes 3145732
  438.7 310.6 %copy-start.8 = (f32[8192]{0:T(1024)}, f32[8192]{0:T(1024)S(1)}, u32[]{:S(2)}) copy-start(f32[8192]{0:T(1024)S(1)} %get-tuple-element.62) | copy-start | bytes 98308
  438.9 310.4 %copy-start.12 = (f32[8192]{0:T(1024)}, f32[8192]{0:T(1024)S(1)}, u32[]{:S(2)}) copy-start(f32[8192]{0:T(1024)S(1)} %log.13) | copy-start | bytes 98308
  604.6 54.9 %copy-start.17 = (s32[8192]{0:T(1024)}, s32[8192]{0:T(1024)S(1)}, u32[]{:S(2)}) copy-start(s32[8192]{0:T(1024)S(1)} %get-tuple-element.24) | copy-start | bytes 98308
  671.0 78.4 %copy-start.6 = (f32[8192,32]{0,1:T(8,128)}, f32[8192,32]{0,1:T(8,128)S(1)}, u32[]{:S(2)}) copy-start(f32[8192,32]{0,1:T(8,128)S(1)} %get-tuple-element.66) | copy-start | bytes 3145732
  671.0 78.4 %copy-start.19 = (f32[8192]{0:T(1024)}, f32[8192]{0:T(1024)S(1)}, u32[]{:S(2)}) copy-start(f32[8192]{0:T(1024)S(1)} %get-tuple-element.12) | copy-start | bytes 98308
  741.3 145.2 %all-to-all-start.2 = ((bf16[32,256,768]{2,1,0:T(8,128)(2,1)}), bf16[32,256,768]{2,1,0:T(8,128)(2,1)}, u32[]{:S(2)}, u32[]{:S(2)}) async-start(bf16[32,256,768]{2,1,0:T(8,128)(2,1)} %broadcast_select_fusion), calls=%async_computation.2 | async-start | bytes 25165824 | tf_op jit(solution)/shard_map/all_to_all | solution.py:80
  746.7 2227.2 %all-reduce.4.cloned.1.call-start = ((), (), s32[]{:S(2)}) async-start(), calls=%async_computation.4 | async-start | bytes 196608 | tf_op jit(solution)/shard_map/psum | solution.py:92
  904.1 51.0 %copy-start.24 = (f32[4,3072]{1,0:T(4,128)S(1)}, f32[4,3072]{1,0:T(4,128)}, u32[]{:S(2)}) copy-start(f32[4,3072]{1,0:T(4,128)} %copy-done.23) | copy-start | bytes 147460
  1184.2 1709.2 %all-to-all-start.3 = ((bf16[4,2048,768]{2,0,1:T(4,128)(2,1)}), bf16[4,2048,768]{2,0,1:T(4,128)(2,1)}, u32[]{:S(2)}, u32[]{:S(2)}) async-start(bf16[4,2048,768]{2,0,1:T(4,128)(2,1)} %copy.52), calls=%async_computation.3 | async-start | bytes 25165824 | tf_op jit(solution)/shard_map/all_to_all | solution.py:89
  2905.1 43.5 %copy-start.5 = (f32[8192,32]{0,1:T(8,128)S(1)}, f32[8192,32]{0,1:T(8,128)}, u32[]{:S(2)}) copy-start(f32[8192,32]{0,1:T(8,128)} %copy-done.4) | copy-start | bytes 3145732
  2905.1 43.5 %copy-start.7 = (f32[8192,32]{0,1:T(8,128)S(1)}, f32[8192,32]{0,1:T(8,128)}, u32[]{:S(2)}) copy-start(f32[8192,32]{0,1:T(8,128)} %copy-done.6) | copy-start | bytes 3145732
  2905.1 43.5 %copy-start.9 = (f32[8192]{0:T(1024)S(1)}, f32[8192]{0:T(1024)}, u32[]{:S(2)}) copy-start(f32[8192]{0:T(1024)} %copy-done.8) | copy-start | bytes 98308
  2905.1 43.5 %copy-start.13 = (f32[8192]{0:T(1024)S(1)}, f32[8192]{0:T(1024)}, u32[]{:S(2)}) copy-start(f32[8192]{0:T(1024)} %copy-done.12) | copy-start | bytes 98308
  2905.2 43.5 %copy-start.20 = (f32[8192]{0:T(1024)S(1)}, f32[8192]{0:T(1024)}, u32[]{:S(2)}) copy-start(f32[8192]{0:T(1024)} %copy-done.19) | copy-start | bytes 98308
  2905.2 43.5 %copy-start.28 = (pred[8192]{0:T(1024)(128)(4,1)S(1)}, pred[8192]{0:T(1024)(128)(4,1)}, u32[]{:S(2)}) copy-start(pred[8192]{0:T(1024)(128)(4,1)} %copy-done.27) | copy-start | bytes 24580
  (13 other events, 199.6 us)
Sparse Core Ops, SparseCore 0:
  759.2 153.3 all-reduce.3
where the time goes:
time: 2990 us; the launch traced here: 2980 us
  blocking collectives  1850 us (62%)
  matrix products  436 us (15%)
  local copies, waits for them, and re-layouts  302 us (10%)
  waiting for transfers between devices  267 us (9%)
  other arithmetic  92.6 us (3%)
    psum x1, blocking collectives, local_step(): expert_grads = lax.psum((d_w_in, d_b_in, d_w_out, d_b_out), 'dp')  1700 us
    psum x1, blocking collectives, local_step(): lax.psum(local_stats, ALL_AXES)  142 us
    all_to_all x1, waiting for transfers between devices, local_step(): recv_rows = lax.all_to_all(send_rows, 'ep', 0, 1, tiled=True)  140 us
    all_to_all x1, waiting for transfers between devices, local_step(): d_recv = lax.all_to_all(d_send, 'ep', 0, 1, tiled=True)  127 us
    dot_general x1, matrix products, local_step(): jnp.einsum('ecw,efw->ecf', d_recv, w_out, preferred_element_type=jnp.floa...  114 us
    dot_general x1, matrix products, local_step(): jnp.einsum('ecw,ewf->ecf', recv_rows, w_in, preferred_element_type=jnp.fl...  74.6 us
  transfers between devices with their start and end apart: 5, of which 2 were waited for; matrix products, arithmetic and copies ran while one was open for 15% of the time, Pallas kernels for 0%

commit v1 on v0

v1 whole, which is shorter than its diff:
```python
import functools

import jax
import jax.numpy as jnp
from jax import lax
from jax.experimental import pallas as pl
from jax.experimental.pallas import tpu as pltpu
from jax.sharding import PartitionSpec as P


ALL_AXES = ("dp", "ep")
PAD_ROWS = 8


def route_tokens(expert_ids, priority, num_experts, capacity, ep_size):
    num_tokens = expert_ids.shape[0]
    local_experts = num_experts // ep_size
    num_slots = num_experts * capacity
    token_iota = jnp.arange(num_tokens, dtype=jnp.int32)
    slot_iota = jnp.arange(num_slots, dtype=jnp.int32)
    span = num_tokens + capacity
    key_tok = expert_ids * span + priority
    key_fill = (slot_iota // capacity) * span + num_tokens + slot_iota % capacity
    item = jnp.concatenate([token_iota, jnp.full((num_slots,), num_tokens, jnp.int32)])
    sorted_key, sorted_item = lax.sort((jnp.concatenate([key_tok, key_fill]), item), num_keys=1, is_stable=False)
    expert_range = jnp.arange(num_experts, dtype=jnp.int32)
    counts = jnp.sum((expert_ids[:, None] == expert_range[None, :]).astype(jnp.int32), axis=0) + capacity
    expert_of = sorted_key // span
    begin = jnp.sum(jnp.where(expert_range[:, None] < expert_of[None, :], counts[:, None], 0), axis=0)
    position = jnp.arange(num_tokens + num_slots, dtype=jnp.int32) - begin
    keep = position < capacity
    slot = ((expert_of % local_experts) * ep_size + expert_of // local_experts) * capacity + jnp.minimum(position, capacity - 1)
    spread = jnp.where(keep, slot, num_slots)
    _, slot_item = lax.sort((spread, sorted_item), num_keys=1, is_stable=False)
    slot_token = slot_item[:num_slots]
    code = slot * 2 + keep.astype(jnp.int32)
    _, token_code = lax.sort((sorted_item, code), num_keys=1, is_stable=False)
    token_code = token_code[:num_tokens]
    return slot_token, token_code // 2, (token_code % 2) == 1


def router_forward(x_loc, modality, router, expert_ids):
    num_experts = router.shape[1]
    logits = jnp.dot(x_loc, router, precision=lax.Precision.HIGHEST, preferred_element_type=jnp.float32)
    log_probs = jax.nn.log_softmax(logits, axis=-1)
    router_probs = jnp.exp(log_probs)
    expert_onehot = (expert_ids[:, None] == jnp.arange(num_experts)[None, :]).astype(jnp.float32)
    gate_prob = jnp.sum(router_probs * expert_onehot, axis=-1)
    mod_mask = jnp.stack([modality == 0, modality == 1]).astype(jnp.float32)
    entropy = -jnp.sum(router_probs * log_probs, axis=-1)
    local_stats = jnp.concatenate([jnp.dot(mod_mask, router_probs), jnp.dot(mod_mask, entropy)[:, None], jnp.sum(mod_mask, axis=1, keepdims=True)], axis=1)
    return log_probs, router_probs, expert_onehot, gate_prob, mod_mask, local_stats


def aux_from_stats(stats, num_experts):
    mod_count = stats[:, num_experts + 1]
    mean_probs = stats[:, :num_experts] / mod_count[:, None]
    aux_loss = jnp.sum(stats[:, num_experts] / mod_count) + jnp.sum(mean_probs * jnp.log(mean_probs))
    return aux_loss, mean_probs, mod_count


def router_backward(x_loc, router, log_probs, router_probs, expert_onehot, mod_mask, mean_probs, mod_count, d_gate):
    inv_count = jnp.dot(1.0 / mod_count, mod_mask)
    global_part = jnp.einsum("mt,me->te", mod_mask, jnp.log(mean_probs) / mod_count[:, None])
    d_probs = expert_onehot * d_gate[:, None] + global_part - log_probs * inv_count[:, None]
    d_logits = router_probs * (d_probs - jnp.sum(d_probs * router_probs, axis=-1, keepdims=True))
    d_router_part = jnp.einsum("tw,te->we", x_loc, d_logits, precision=lax.Precision.HIGHEST, preferred_element_type=jnp.float32)
    dx_router = jnp.einsum("te,we->tw", d_logits, router, precision=lax.Precision.HIGHEST, preferred_element_type=jnp.float32)
    return d_router_part, dx_router.astype(jnp.bfloat16)


GELU_A = 0.7978845608028654
GELU_B = 0.044715 * GELU_A
NT = (((1,), (1,)), ((), ()))
NN = (((1,), (0,)), ((), ()))


def mm(lhs, rhs, dims=NN):
    return lax.dot_general(lhs, rhs, dims, preferred_element_type=jnp.float32)


def gelu_and_slope(act):
    sq = act * act
    gate = 0.5 * jnp.tanh(act * (GELU_B * sq + GELU_A)) + 0.5
    value = act * gate
    slope = gate + value * (1.0 - gate) * (6.0 * GELU_B * sq + 2.0 * GELU_A)
    return value, slope


def act_tile(x_rows, d_rows, w_in, bias, w_out):
    act = mm(x_rows, w_in) + bias
    d_hidden = mm(d_rows, w_out, NT).astype(jnp.bfloat16).astype(jnp.float32)
    value, slope = gelu_and_slope(act)
    return value.astype(jnp.bfloat16), d_hidden * slope


def own_kernel(tile, sub, rows_ref, w_in_ref, b_in_ref, w_out_ref, b_out_ref, both_ref, hidden_ref, dact_ref, dbias_ref):
    count = rows_ref.shape[0]
    width = w_in_ref.shape[0]
    hidden_size = w_in_ref.shape[1]

    @pl.when(pl.program_id(0) == 0)
    def _():
        dbias_ref[...] = jnp.zeros_like(dbias_ref)

    def hidden_step(step, carry):
        for part in range(tile // sub):
            cols = pl.ds(pl.multiple_of(step * tile + part * sub, sub), sub)
            total = jnp.zeros((1, sub), jnp.float32)
            for start in range(0, count, sub):
                block = slice(start, start + sub)
                value, d_act = act_tile(rows_ref[block, :width], rows_ref[block, width:], w_in_ref[:, cols], b_in_ref[:, cols].astype(jnp.float32), w_out_ref[cols, :])
                hidden_ref[block, cols] = value
                dact_ref[block, cols] = d_act.astype(jnp.bfloat16)
                total = total + jnp.sum(d_act, axis=0, keepdims=True)
            dbias_ref[:, cols] += total
        return carry

    lax.fori_loop(0, hidden_size // tile, hidden_step, 0)

    def out_step(step, carry):
        cols = pl.ds(pl.multiple_of(step * sub, sub), sub)
        back = pl.ds(pl.multiple_of(width + step * sub, sub), sub)
        both_ref[:, cols] = (mm(hidden_ref[...], w_out_ref[:, cols]) + b_out_ref[:, cols].astype(jnp.float32)).astype(jnp.bfloat16)
        both_ref[:, back] = mm(dact_ref[...], w_in_ref[cols, :], NT).astype(jnp.bfloat16)
        return carry

    lax.fori_loop(0, width // sub, out_step, 0)


def own_call(index, rows, w_in, b_in, w_out, b_out, block=512):
    num_rows, wide = rows.shape
    width = wide // 2
    hidden_size = w_in.shape[2]
    whole = lambda shape: pl.BlockSpec((None,) + shape, lambda i: (index, 0, 0), pipeline_mode=pl.Buffered(1))
    flops = 8 * num_rows * width * hidden_size
    return pl.pallas_call(
        functools.partial(own_kernel, 512, 256),
        grid=(num_rows // block,),
        in_specs=[
            pl.BlockSpec((block, wide), lambda i: (i, 0)),
            whole((width, hidden_size)),
            whole((1, hidden_size)),
            whole((hidden_size, width)),
            whole((1, width)),
        ],
        out_specs=[
            pl.BlockSpec((block, wide), lambda i: (i, 0)),
            pl.BlockSpec((block, hidden_size), lambda i: (i, 0)),
            pl.BlockSpec((block, hidden_size), lambda i: (i, 0)),
            pl.BlockSpec((1, hidden_size), lambda i: (0, 0)),
        ],
        out_shape=[
            jax.ShapeDtypeStruct((num_rows, wide), jnp.bfloat16),
            jax.ShapeDtypeStruct((num_rows, hidden_size), jnp.bfloat16),
            jax.ShapeDtypeStruct((num_rows, hidden_size), jnp.bfloat16),
            jax.ShapeDtypeStruct((1, hidden_size), jnp.float32),
        ],
        compiler_params=pltpu.CompilerParams(dimension_semantics=("arbitrary",), vmem_limit_bytes=60 * 2**20),
        cost_estimate=pl.CostEstimate(flops=flops, bytes_accessed=8 * num_rows * hidden_size, transcendentals=num_rows * hidden_size),
        name="expert_own",
    )(rows, w_in, b_in[:, None, :], w_out, b_out[:, None, :])


def grad_kernel(sub, own_ref, other_ref, hidden_ref, dact_ref, dbias_ref, w_in_ref, b_in_ref, w_out_ref, *refs):
    dw_in_ref, db_in_ref, dw_out_ref, db_out_ref, xt_ref, dt_ref, h_ref, a_ref = refs[-8:]
    half = own_ref.shape[0]
    width = own_ref.shape[1] // 2
    tile = w_in_ref.shape[1]

    @pl.when(pl.program_id(0) == 0)
    def _():
        def flip(step, total):
            for ref, base in ((own_ref, 0), (other_ref, half)):
                block = pl.ds(pl.multiple_of(step * sub, sub), sub)
                cols = pl.ds(pl.multiple_of(base + step * sub, sub), sub)
                d_rows = ref[block, width:]
                xt_ref[:, cols] = ref[block, :width].T
                dt_ref[:, cols] = d_rows.T
                total = total + jnp.sum(d_rows.astype(jnp.float32), axis=0, keepdims=True)
            return total

        total = lax.fori_loop(0, half // sub, flip, jnp.zeros((1, width), jnp.float32))
        db_out_ref[...] = total.astype(jnp.bfloat16)

    def remote_step(step, total):
        block = pl.ds(pl.multiple_of(step * sub, sub), sub)
        parts = []
        for start in range(0, tile, sub):
            cols = slice(start, start + sub)
            value, d_act = act_tile(other_ref[block, :width], other_ref[block, width:], w_in_ref[:, cols], b_in_ref[:, cols].astype(jnp.float32), w_out_ref[cols, :])
            h_ref[block, cols] = value
            a_ref[block, cols] = d_act.astype(jnp.bfloat16)
            parts.append(jnp.sum(d_act, axis=0, keepdims=True))
        return total + jnp.concatenate(parts, axis=1)

    total = lax.fori_loop(0, half // sub, remote_step, dbias_ref[...])
    db_in_ref[...] = total.astype(jnp.bfloat16)

    def grad_step(step, carry):
        cols = pl.ds(pl.multiple_of(step * sub, sub), sub)
        d_in = mm(xt_ref[:, :half], dact_ref[:, cols]) + mm(xt_ref[:, half:], a_ref[:, cols])
        dw_in_ref[:, cols] = d_in.astype(jnp.bfloat16)
        d_out = mm(dt_ref[:, :half], hidden_ref[:, cols]) + mm(dt_ref[:, half:], h_ref[:, cols])
        dw_out_ref[cols, :] = d_out.T.astype(jnp.bfloat16)
        return carry

    lax.fori_loop(0, tile // sub, grad_step, 0)


def grad_call(index, own, other, hidden, dact, dbias, w_in, b_in, w_out, partial_grads, tile=512, sub=256):
    num_rows, wide = own.shape
    experts, width, hidden_size = w_in.shape
    resident = pl.BlockSpec((num_rows, wide), lambda i: (0, 0), pipeline_mode=pl.Buffered(1))
    saved = pl.BlockSpec((num_rows, tile), lambda i: (0, i))
    in_specs = [
        resident,
        resident,
        saved,
        saved,
        pl.BlockSpec((1, tile), lambda i: (0, i)),
        pl.BlockSpec((None, width, tile), lambda i: (index, 0, i)),
        pl.BlockSpec((None, 1, tile), lambda i: (index, 0, i)),
        pl.BlockSpec((None, tile, width), lambda i: (index, i, 0)),
    ]
    operands = [own, other, hidden, dact, dbias, w_in, b_in[:, None, :], w_out]
    aliases = {}
    if partial_grads is not None:
        for place, grad in enumerate(partial_grads):
            aliases[len(operands)] = place
            operands.append(grad)
            in_specs.append(pl.BlockSpec(memory_space=pl.ANY))
    flops = 12 * num_rows * width * hidden_size
    return pl.pallas_call(
        functools.partial(grad_kernel, sub),
        grid=(hidden_size // tile,),
        in_specs=in_specs,
        out_specs=[
            pl.BlockSpec((None, width, tile), lambda i: (index, 0, i)),
            pl.BlockSpec((None, 1, tile), lambda i: (index, 0, i)),
            pl.BlockSpec((None, tile, width), lambda i: (index, i, 0)),
            pl.BlockSpec((None, 1, width), lambda i: (index, 0, 0)),
        ],
        out_shape=[
            jax.ShapeDtypeStruct((experts, width, hidden_size), jnp.bfloat16),
            jax.ShapeDtypeStruct((experts, 1, hidden_size), jnp.bfloat16),
            jax.ShapeDtypeStruct((experts, hidden_size, width), jnp.bfloat16),
            jax.ShapeDtypeStruct((experts, 1, width), jnp.bfloat16),
        ],
        scratch_shapes=[
            pltpu.VMEM((width, 2 * num_rows), jnp.bfloat16),
            pltpu.VMEM((width, 2 * num_rows), jnp.bfloat16),
            pltpu.VMEM((num_rows, tile), jnp.bfloat16),
            pltpu.VMEM((num_rows, tile), jnp.bfloat16),
        ],
        input_output_aliases=aliases,
        compiler_params=pltpu.CompilerParams(dimension_semantics=("arbitrary",), vmem_limit_bytes=60 * 2**20),
        cost_estimate=pl.CostEstimate(flops=flops, bytes_accessed=8 * num_rows * hidden_size, transcendentals=num_rows * hidden_size),
        name="expert_grad",
    )(*operands)


def solution(mesh):
    token_spec = P(ALL_AXES)
    expert_spec = P("ep")
    ep_size = mesh.shape["ep"]

    def local_step(x_loc, modality, router, expert_ids, priority, w_in, b_in, w_out, b_out, dy_loc):
        num_tokens, width = x_loc.shape
        num_experts = router.shape[1]
        local_experts = w_in.shape[0]
        capacity = num_tokens // num_experts
        chunk = ep_size * capacity
        slot_token, token_slot, keep_mask = route_tokens(expert_ids, priority, num_experts, capacity, ep_size)
        log_probs, router_probs, expert_onehot, gate_prob, mod_mask, local_stats = router_forward(x_loc, modality, router, expert_ids)
        stats = lax.psum(local_stats, ALL_AXES)
        aux_loss, mean_probs, mod_count = aux_from_stats(stats, num_experts)
        dy_f32 = dy_loc.astype(jnp.float32)
        d_ytok = (gate_prob[:, None] * dy_f32).astype(jnp.bfloat16)
        source = jnp.pad(jnp.concatenate([x_loc, d_ytok], axis=1), ((0, PAD_ROWS), (0, 0)))

        source, aux_loss = lax.optimization_barrier((source, aux_loss))

        own, other = [], []
        for j in range(local_experts):
            send = source[slot_token[j * chunk:(j + 1) * chunk]].reshape(ep_size, capacity, 2 * width)
            got = lax.all_to_all(send, "ep", 0, 0, tiled=True).reshape(chunk, 2 * width)
            own.append(got)
            other.append(lax.ppermute(got, "dp", [(0, 1), (1, 0)]))
        back = []
        kept = []
        for j in range(local_experts):
            both, hidden, d_act, d_bias = own_call(j, own[j], w_in, b_in, w_out, b_out)
            back.append(lax.all_to_all(both.reshape(ep_size, capacity, 2 * width), "ep", 0, 0, tiled=True).reshape(chunk, 2 * width))
            kept.append((hidden, d_act, d_bias))
        expert_grads = None
        for j in range(local_experts):
            expert_grads = grad_call(j, own[j], other[j], *kept[j], w_in, b_in, w_out, expert_grads)
        d_w_in, d_b_in, d_w_out, d_b_out = expert_grads
        expert_grads = (d_w_in, d_b_in[:, 0], d_w_out, d_b_out[:, 0])

        tok_rows = jnp.concatenate(back, axis=0)[token_slot]
        keep_col = keep_mask[:, None]
        y_tok = tok_rows[:, :width].astype(jnp.float32)
        out_tokens = jnp.where(keep_col, gate_prob[:, None] * y_tok, 0.0).astype(jnp.bfloat16)
        d_gate = jnp.where(keep_mask, jnp.sum(dy_f32 * y_tok, axis=-1), 0.0)
        dx_expert = jnp.where(keep_col, tok_rows[:, width:], 0).astype(jnp.bfloat16)
        d_router_part, dx_router = router_backward(x_loc, router, log_probs, router_probs, expert_onehot, mod_mask, mean_probs, mod_count, d_gate)
        d_router = lax.psum(d_router_part, ALL_AXES)
        return (out_tokens, aux_loss, dx_expert + dx_router, d_router) + tuple(expert_grads)

    return jax.shard_map(
        local_step,
        mesh=mesh,
        in_specs=(token_spec, token_spec, P(), token_spec, token_spec, expert_spec, expert_spec, expert_spec, expert_spec, token_spec),
        out_specs=(token_spec, P(), token_spec, P(), expert_spec, expert_spec, expert_spec, expert_spec),
        check_vma=False,
    )
```

time: 2990 us -> 1340 us (0.45)
  blocking collectives: 1850 us -> 34.6 us
  Pallas kernels: 0 us -> 619 us
  matrix products: 436 us -> 47.6 us
  local copies, waits for them, and re-layouts: 302 us -> 166 us
  waiting for transfers between devices: 267 us -> 300 us
    psum x2 -> x1, blocking collectives: 1850 us -> 34.6 us  [local_step(): stats = lax.psum(local_stats, ALL_AXES)]
    pallas_call x0 -> x8, Pallas kernels: none -> 619 us  [the longest x4 362 us: grad_call(): pl.pallas_call(functools.partial(grad_kernel, sub), grid=(hidden_size //...]
    dot_general x6 -> x0, matrix products: 386 us -> none  [the longest x1 114 us: local_step(): jnp.einsum('ecw,efw->ecf', d_recv, w_out, preferred_element_type=jnp.floa...]
    ppermute x0 -> x4, waiting for transfers between devices: none -> 71.6 us  [local_step(): other.append(lax.ppermute(got, 'dp', [(0, 1), (1, 0)]))]
    gather x8 -> x5, local copies, waits for them, and re-layouts: 220 us -> 159 us  [the longest x4 98.6 us: local_step(): source[slot_token[j * chunk:(j + 1) * chunk]]]
    all_to_all x4 -> x0, local copies, waits for them, and re-layouts: 44.7 us -> none  [the longest x1 11.7 us: local_step(): lax.all_to_all(expert_out.astype(jnp.bfloat16), 'ep', 1, 0, tiled=True)]
    concatenate x0 -> x3, other arithmetic: none -> 44.2 us  [the longest x1 25.3 us: local_step(): jnp.concatenate([x_loc, d_ytok], axis=1)]
    all_to_all x4 -> x8, waiting for transfers between devices: 267 us -> 228 us  [the longest x4 147 us: local_step(): got = lax.all_to_all(send, 'ep', 0, 0, tiled=True).reshape(chunk, 2 * width)]
  transfers between devices with their start and end apart: 5 -> 13, of which waited for: 2 -> 10; matrix products, arithmetic and copies ran while one was open for 15% -> 17% of each run, Pallas kernels for 0% -> 46%
where the time goes in v1:
time: 1340 us
  Pallas kernels  619 us (46%)
  waiting for transfers between devices  300 us (22%)
  local copies, waits for them, and re-layouts  166 us (12%)
  other arithmetic  108 us (8%)
  matrix products  47.6 us (4%)
  starting transfers between devices  43.4 us (3%)
  blocking collectives  34.6 us (3%)
  between operations  17.2 us (1%)
    pallas_call x4, Pallas kernels, grad_call(): pl.pallas_call(functools.partial(grad_kernel, sub), grid=(hidden_size //...  362 us
    pallas_call x4, Pallas kernels, own_call(): pl.pallas_call(functools.partial(own_kernel, 512, 256), grid=(num_rows //...  257 us
    all_to_all x4, waiting for transfers between devices, local_step(): got = lax.all_to_all(send, 'ep', 0, 0, tiled=True).reshape(chunk, 2 * width)  147 us
    gather x4, local copies, waits for them, and re-layouts, local_step(): source[slot_token[j * chunk:(j + 1) * chunk]]  98.6 us
    all_to_all x4, waiting for transfers between devices, local_step(): lax.all_to_all(both.reshape(ep_size, capacity, 2 * width), 'ep', 0, 0, ti...  81.4 us
    ppermute x4, waiting for transfers between devices, local_step(): other.append(lax.ppermute(got, 'dp', [(0, 1), (1, 0)]))  71.6 us
    gather x1, local copies, waits for them, and re-layouts, local_step(): tok_rows = jnp.concatenate(back, axis=0)[token_slot]  60.7 us
    psum x1, blocking collectives, local_step(): stats = lax.psum(local_stats, ALL_AXES)  34.6 us
  transfers between devices with their start and end apart: 13, of which 10 were waited for; matrix products, arithmetic and copies ran while one was open for 17% of the time, Pallas kernels for 46%

profile of v1, /device:TPU:0, one launch (start us, length us, event | category | flops | bytes accessed | tf_op | source)
XLA Modules:
  0.0 1335.1 jit_solution(7526559738921056681)
XLA Ops:
  25.9 13.9 %fusion.50 = (f32[8192]{0:T(1024)S(1)}, f32[8192,32]{0,1:T(8,128)S(1)}) fusion(bf16[8192,768]{1,0:T(8,128)(2,1)} %param.10, f32[768,32]{0,1:T(8,128)S(1)} %copy-done), kind=kOutput, calls=%fused_computation.118 | convolution fusion | flops 2416173056 | bytes 13762560 | tf_op jit(solution)/shard_map/dot_general | solution.py:44
  41.4 34.6 %psum.14 = f32[2,34]{1,0:T(2,128)S(1)} all-reduce(f32[2,34]{1,0:T(2,128)S(1)} %pad_maximum_fusion.1), channel_id=1, replica_groups=mesh['dp'=2,'ep'=8] {'dp','ep'}, use_global_device_ids=true, to_apply=%region_9.10 | all-reduce | flops 68 | bytes 544 | tf_op jit(solution)/shard_map/psum | solution.py:276
  89.2 25.3 %fusion.2 = bf16[8200,1536]{1,0:T(8,128)(2,1)} fusion(bf16[8192,768]{1,0:T(8,128)(2,1)} %fusion.3, bf16[8192,768]{1,0:T(8,128)(2,1)} %param.10), kind=kLoop, calls=%fused_computation.11 | loop fusion | flops 88166400 | bytes 50356224 | tf_op jit(solution)/shard_map/concatenate | solution.py:280
  115.9 24.7 %gather_fusion.3 = bf16[2048,1536]{1,0:T(8,128)(2,1)} fusion(bf16[8200,1536]{1,0:T(8,128)(2,1)} %fusion.2, s32[2048]{0:T(1024)S(1)} %get-tuple-element.98), kind=kCustom, calls=%fused_computation.3 | custom fusion | bytes 12591104 | tf_op jit(solution)/shard_map/gather | solution.py:286
  145.5 24.7 %gather_fusion.2 = bf16[2048,1536]{1,0:T(8,128)(2,1)} fusion(bf16[8200,1536]{1,0:T(8,128)(2,1)} %fusion.2, s32[2048]{0:T(1024)S(1)} %get-tuple-element.99), kind=kCustom, calls=%fused_computation.2 | custom fusion | bytes 12591104 | tf_op jit(solution)/shard_map/gather | solution.py:286
  170.2 46.9 %all-to-all-done.6 = bf16[8,256,1536]{2,1,0:T(8,128)(2,1)} async-done(((bf16[8,256,1536]{2,1,0:T(8,128)(2,1)}), bf16[8,256,1536]{2,1,0:T(8,128)(2,1)}, u32[]{:S(2)}, u32[]{:S(2)}) %all-to-all-start.6) | async-done | bytes 6291488 | tf_op jit(solution)/shard_map/all_to_all | solution.py:287
  221.9 24.7 %gather_fusion = bf16[2048,1536]{1,0:T(8,128)(2,1)} fusion(bf16[8200,1536]{1,0:T(8,128)(2,1)} %fusion.2, s32[2048]{0:T(1024)S(1)} %get-tuple-element.97), kind=kCustom, calls=%fused_computation | custom fusion | bytes 12591104 | tf_op jit(solution)/shard_map/gather | solution.py:286
  246.5 46.9 %all-to-all-done.4 = bf16[8,256,1536]{2,1,0:T(8,128)(2,1)} async-done(((bf16[8,256,1536]{2,1,0:T(8,128)(2,1)}), bf16[8,256,1536]{2,1,0:T(8,128)(2,1)}, u32[]{:S(2)}, u32[]{:S(2)}) %all-to-all-start.4) | async-done | bytes 6291488 | tf_op jit(solution)/shard_map/all_to_all | solution.py:287
  298.6 24.7 %gather_fusion.1 = bf16[2048,1536]{1,0:T(8,128)(2,1)} fusion(bf16[8200,1536]{1,0:T(8,128)(2,1)} %fusion.2, s32[2048]{0:T(1024)S(1)} %get-tuple-element.100), kind=kCustom, calls=%fused_computation.1 | custom fusion | bytes 12591104 | tf_op jit(solution)/shard_map/gather | solution.py:286
  323.3 46.9 %all-to-all-done = bf16[8,256,1536]{2,1,0:T(8,128)(2,1)} async-done(((bf16[8,256,1536]{2,1,0:T(8,128)(2,1)}), bf16[8,256,1536]{2,1,0:T(8,128)(2,1)}, u32[]{:S(2)}, u32[]{:S(2)}) %all-to-all-start) | async-done | bytes 6291488 | tf_op jit(solution)/shard_map/all_to_all | solution.py:287
  376.3 64.2 %expert_own.4 = (bf16[2048,1536]{1,0:T(8,128)(2,1)}, bf16[2048,3072]{1,0:T(8,128)(2,1)}, bf16[2048,3072]{1,0:T(8,128)(2,1)}, f32[1,3072]{1,0:T(1,128)}) custom-call(bf16[2048,1536]{1,0:T(8,128)(2,1)} %bitcast.5.rows_ref.own_ref, bf16[4,768,3072]{2,1,0:T(8,128)(2,1)} %w_in_ref.15, bf16[4,1,3072]{2,1,0:T(2,128)(2,1)} %copy.48.b_in_ref, ...), custom_call_target="tpu_custom_call" | custom-call | flops 38654705664 | bytes 50331648 | tf_op jit(solution)/shard_map/expert_own/pallas_call | solution.py:137
  451.4 64.4 %expert_own.5 = (bf16[2048,1536]{1,0:T(8,128)(2,1)}, bf16[2048,3072]{1,0:T(8,128)(2,1)}, bf16[2048,3072]{1,0:T(8,128)(2,1)}, f32[1,3072]{1,0:T(1,128)}) custom-call(bf16[2048,1536]{1,0:T(8,128)(2,1)} %bitcast.11.rows_ref.own_ref, bf16[4,768,3072]{2,1,0:T(8,128)(2,1)} %w_in_ref.15, bf16[4,1,3072]{2,1,0:T(2,128)(2,1)} %copy.48.b_in_ref, ...), custom_call_target="tpu_custom_call" | custom-call | flops 38654705664 | bytes 50331648 | tf_op jit(solution)/shard_map/expert_own/pallas_call | solution.py:137
  527.9 64.3 %expert_own.6 = (bf16[2048,1536]{1,0:T(8,128)(2,1)}, bf16[2048,3072]{1,0:T(8,128)(2,1)}, bf16[2048,3072]{1,0:T(8,128)(2,1)}, f32[1,3072]{1,0:T(1,128)}) custom-call(bf16[2048,1536]{1,0:T(8,128)(2,1)} %bitcast.15.rows_ref.own_ref, bf16[4,768,3072]{2,1,0:T(8,128)(2,1)} %w_in_ref.15, bf16[4,1,3072]{2,1,0:T(2,128)(2,1)} %copy.48.b_in_ref, ...), custom_call_target="tpu_custom_call" | custom-call | flops 38654705664 | bytes 50331648 | tf_op jit(solution)/shard_map/expert_own/pallas_call | solution.py:137
  604.3 64.3 %expert_own.7 = (bf16[2048,1536]{1,0:T(8,128)(2,1)}, bf16[2048,3072]{1,0:T(8,128)(2,1)}, bf16[2048,3072]{1,0:T(8,128)(2,1)}, f32[1,3072]{1,0:T(1,128)}) custom-call(bf16[2048,1536]{1,0:T(8,128)(2,1)} %bitcast.19.rows_ref.own_ref, bf16[4,768,3072]{2,1,0:T(8,128)(2,1)} %w_in_ref.15, bf16[4,1,3072]{2,1,0:T(2,128)(2,1)} %copy.48.b_in_ref, ...), custom_call_target="tpu_custom_call" | custom-call | flops 38654705664 | bytes 50331648 | tf_op jit(solution)/shard_map/expert_own/pallas_call | solution.py:137
  692.4 59.8 %all-to-all-done.7 = bf16[8,256,1536]{2,1,0:T(8,128)(2,1)} async-done(((bf16[8,256,1536]{2,1,0:T(8,128)(2,1)}), bf16[8,256,1536]{2,1,0:T(8,128)(2,1)}, u32[]{:S(2)}, u32[]{:S(2)}) %all-to-all-start.7) | async-done | bytes 6291488 | tf_op jit(solution)/shard_map/all_to_all | solution.py:294
  752.2 18.9 %pad_maximum_fusion = bf16[8192,1536]{1,0:T(8,128)(2,1)} fusion(bf16[2048,1536]{1,0:T(8,128)(2,1)} %bitcast.21, bf16[2048,1536]{1,0:T(8,128)(2,1)} %bitcast.17, bf16[2048,1536]{1,0:T(8,128)(2,1)} %bitcast.13, bf16[2048,1536]{1,0:T(8,128)(2,1)} %bitcast.9), kind=kLoop, calls=%fused_computation.16 | loop fusion | flops 100663296 | bytes 50331648 | tf_op jit(solution)/shard_map/concatenate | solution.py:302
  771.1 60.7 %gather_fusion.4 = bf16[8192,1536]{1,0:T(8,128)(2,1)} fusion(bf16[8192,1536]{1,0:T(8,128)(2,1)} %pad_maximum_fusion, s32[8192]{0:T(1024)S(1)} %get-tuple-element.90), kind=kCustom, calls=%fused_computation.4 | custom fusion | bytes 50364416 | tf_op jit(solution)/shard_map/gather | solution.py:302
  856.6 25.7 %fusion.7 = bf16[8192,768]{1,0:T(8,128)(2,1)} fusion(bf16[8192,1536]{1,0:T(8,128)(2,1)} %gather_fusion.4, pred[8192]{0:T(1024)(128)(4,1)S(1)} %get-tuple-element.89, f32[768,32]{0,1:T(8,128)S(1)} %copy-done, f32[8192,32]{0,1:T(8,128)S(1)} %get-tuple-element.106, f32[8192]{0:T(1024)S(1)} %get-tuple-element.105, f32[8192,32]{0,1:T(8,128)S(1)} %copy-done.3, ...), kind=kOutput, calls=%fused_computation.19 | convolution fusion | flops 2435842048 | bytes 27467776 | tf_op jit(solution)/shard_map/te,we->tw/dot_general | solution.py:68
  889.0 90.6 %expert_grad.4 = (bf16[4,768,3072]{2,1,0:T(8,128)(2,1)}, bf16[4,1,3072]{2,1,0:T(2,128)(2,1)}, bf16[4,3072,768]{2,1,0:T(8,128)(2,1)}, bf16[4,1,768]{2,1,0:T(2,128)(2,1)}) custom-call(bf16[2048,1536]{1,0:T(8,128)(2,1)} %bitcast.5.rows_ref.own_ref, bf16[2048,1536]{1,0:T(8,128)(2,1)} %collective-permute-done.3.other_ref, ...), custom_call_target="tpu_custom_call" | custom-call | flops 57982058496 | bytes 50331648 | tf_op jit(solution)/shard_map/expert_grad/pallas_call | solution.py:234
  979.6 90.4 %expert_grad.5 = (bf16[4,768,3072]{2,1,0:T(8,128)(2,1)}, bf16[4,1,3072]{2,1,0:T(2,128)(2,1)}, bf16[4,3072,768]{2,1,0:T(8,128)(2,1)}, bf16[4,1,768]{2,1,0:T(2,128)(2,1)}) custom-call(bf16[2048,1536]{1,0:T(8,128)(2,1)} %bitcast.11.rows_ref.own_ref, ...), custom_call_target="tpu_custom_call", output_to_operand_aliasing={{0}: (8, {}), {1}: (9, {}), {2}: (10, {}), {3}: (11, {})} | custom-call | flops 57982058496 | bytes 50331648 | tf_op jit(solution)/shard_map/expert_grad/pallas_call | solution.py:234
  1070.0 27.5 %collective-permute-done.1.other_ref = bf16[2048,1536]{1,0:T(8,128)(2,1)} collective-permute-done((bf16[2048,1536]{1,0:T(8,128)(2,1)}, bf16[2048,1536]{1,0:T(8,128)(2,1)}, u32[]{:S(2)}, u32[]{:S(2)}) %collective-permute-start.1) | collective-permute-done | bytes 6291488 | tf_op jit(solution)/shard_map/ppermute | solution.py:289
  1097.5 90.4 %expert_grad.6 = (bf16[4,768,3072]{2,1,0:T(8,128)(2,1)}, bf16[4,1,3072]{2,1,0:T(2,128)(2,1)}, bf16[4,3072,768]{2,1,0:T(8,128)(2,1)}, bf16[4,1,768]{2,1,0:T(2,128)(2,1)}) custom-call(bf16[2048,1536]{1,0:T(8,128)(2,1)} %bitcast.15.rows_ref.own_ref, ...), custom_call_target="tpu_custom_call", output_to_operand_aliasing={{0}: (8, {}), {1}: (9, {}), {2}: (10, {}), {3}: (11, {})} | custom-call | flops 57982058496 | bytes 50331648 | tf_op jit(solution)/shard_map/expert_grad/pallas_call | solution.py:234
  1187.9 44.1 %collective-permute-done.other_ref = bf16[2048,1536]{1,0:T(8,128)(2,1)} collective-permute-done((bf16[2048,1536]{1,0:T(8,128)(2,1)}, bf16[2048,1536]{1,0:T(8,128)(2,1)}, u32[]{:S(2)}, u32[]{:S(2)}) %collective-permute-start) | collective-permute-done | bytes 6291488 | tf_op jit(solution)/shard_map/ppermute | solution.py:289
  1232.0 90.6 %expert_grad.7 = (bf16[4,768,3072]{2,1,0:T(8,128)(2,1)}, bf16[4,1,3072]{2,1,0:T(2,128)(2,1)}, bf16[4,3072,768]{2,1,0:T(8,128)(2,1)}, bf16[4,1,768]{2,1,0:T(2,128)(2,1)}) custom-call(bf16[2048,1536]{1,0:T(8,128)(2,1)} %bitcast.19.rows_ref.own_ref, ...), custom_call_target="tpu_custom_call", output_to_operand_aliasing={{0}: (8, {}), {1}: (9, {}), {2}: (10, {}), {3}: (11, {})} | custom-call | flops 57982058496 | bytes 50331648 | tf_op jit(solution)/shard_map/expert_grad/pallas_call | solution.py:234
  (116 shorter events, 148.6 us)
Async XLA Ops:
  7.2 32.9 %copy-start.10 = (s32[8192]{0:T(1024)S(1)}, s32[8192]{0:T(1024)}, u32[]{:S(2)}) copy-start(s32[8192]{0:T(1024)} %param.13) | copy-start | bytes 98308
  9.3 79.9 %copy-start.16 = (pred[2,8192]{1,0:T(4,128)(4,1)}, pred[2,8192]{1,0:T(4,128)(4,1)S(1)}, u32[]{:S(2)}) copy-start(pred[2,8192]{1,0:T(4,128)(4,1)S(1)} %get-tuple-element.96) | copy-start | bytes 49156
  17.5 71.7 %copy-start.13 = (s32[16384]{0:T(1024)}, s32[16384]{0:T(1024)S(1)}, u32[]{:S(2)}) copy-start(s32[16384]{0:T(1024)S(1)} %get-tuple-element.46) | copy-start | bytes 196612
  40.6 48.6 %copy-start.8 = (f32[8192]{0:T(1024)}, f32[8192]{0:T(1024)S(1)}, u32[]{:S(2)}) copy-start(f32[8192]{0:T(1024)S(1)} %get-tuple-element.85) | copy-start | bytes 98308
  140.5 76.6 %all-to-all-start.6 = ((bf16[8,256,1536]{2,1,0:T(8,128)(2,1)}), bf16[8,256,1536]{2,1,0:T(8,128)(2,1)}, u32[]{:S(2)}, u32[]{:S(2)}) async-start(bf16[8,256,1536]{2,1,0:T(8,128)(2,1)} %bitcast.50), calls=%async_computation.6 | async-start | bytes 12582912 | tf_op jit(solution)/shard_map/all_to_all | solution.py:287
  217.1 76.3 %all-to-all-start.4 = ((bf16[8,256,1536]{2,1,0:T(8,128)(2,1)}), bf16[8,256,1536]{2,1,0:T(8,128)(2,1)}, u32[]{:S(2)}, u32[]{:S(2)}) async-start(bf16[8,256,1536]{2,1,0:T(8,128)(2,1)} %bitcast.49), calls=%async_computation.4 | async-start | bytes 12582912 | tf_op jit(solution)/shard_map/all_to_all | solution.py:287
  293.4 76.7 %all-to-all-start = ((bf16[8,256,1536]{2,1,0:T(8,128)(2,1)}), bf16[8,256,1536]{2,1,0:T(8,128)(2,1)}, u32[]{:S(2)}, u32[]{:S(2)}) async-start(bf16[8,256,1536]{2,1,0:T(8,128)(2,1)} %bitcast.48), calls=%async_computation | async-start | bytes 12582912 | tf_op jit(solution)/shard_map/all_to_all | solution.py:287
  323.3 51.8 %copy-start.21 = (bf16[4,768]{1,0:T(4,128)(2,1)S(1)}, bf16[4,768]{1,0:T(4,128)(2,1)}, u32[]{:S(2)}) copy-start(bf16[4,768]{1,0:T(4,128)(2,1)} %param.18) | copy-start | bytes 18436
  323.3 52.4 %copy-start.18 = (bf16[4,3072]{1,0:T(4,128)(2,1)S(1)}, bf16[4,3072]{1,0:T(4,128)(2,1)}, u32[]{:S(2)}) copy-start(bf16[4,3072]{1,0:T(4,128)(2,1)} %param.16) | copy-start | bytes 73732
  370.2 76.4 %all-to-all-start.2 = ((bf16[8,256,1536]{2,1,0:T(8,128)(2,1)}), bf16[8,256,1536]{2,1,0:T(8,128)(2,1)}, u32[]{:S(2)}, u32[]{:S(2)}) async-start(bf16[8,256,1536]{2,1,0:T(8,128)(2,1)} %bitcast.47), calls=%async_computation.2 | async-start | bytes 12582912 | tf_op jit(solution)/shard_map/all_to_all | solution.py:287
  446.6 76.4 %all-to-all-start.1 = ((bf16[8,256,1536]{2,1,0:T(8,128)(2,1)}), bf16[8,256,1536]{2,1,0:T(8,128)(2,1)}, u32[]{:S(2)}, u32[]{:S(2)}) async-start(bf16[8,256,1536]{2,1,0:T(8,128)(2,1)} %bitcast.53), calls=%async_computation.1 | async-start | bytes 12582912 | tf_op jit(solution)/shard_map/all_to_all | solution.py:294
  523.0 76.5 %all-to-all-start.3 = ((bf16[8,256,1536]{2,1,0:T(8,128)(2,1)}), bf16[8,256,1536]{2,1,0:T(8,128)(2,1)}, u32[]{:S(2)}, u32[]{:S(2)}) async-start(bf16[8,256,1536]{2,1,0:T(8,128)(2,1)} %bitcast.54), calls=%async_computation.3 | async-start | bytes 12582912 | tf_op jit(solution)/shard_map/all_to_all | solution.py:294
  599.5 76.3 %all-to-all-start.5 = ((bf16[8,256,1536]{2,1,0:T(8,128)(2,1)}), bf16[8,256,1536]{2,1,0:T(8,128)(2,1)}, u32[]{:S(2)}, u32[]{:S(2)}) async-start(bf16[8,256,1536]{2,1,0:T(8,128)(2,1)} %bitcast.52), calls=%async_computation.5 | async-start | bytes 12582912 | tf_op jit(solution)/shard_map/all_to_all | solution.py:294
  668.6 19.2 %copy-start.17 = (pred[2,8192]{1,0:T(4,128)(4,1)S(1)}, pred[2,8192]{1,0:T(4,128)(4,1)}, u32[]{:S(2)}) copy-start(pred[2,8192]{1,0:T(4,128)(4,1)} %copy-done.16) | copy-start | bytes 49156
  675.8 76.3 %all-to-all-start.7 = ((bf16[8,256,1536]{2,1,0:T(8,128)(2,1)}), bf16[8,256,1536]{2,1,0:T(8,128)(2,1)}, u32[]{:S(2)}, u32[]{:S(2)}) async-start(bf16[8,256,1536]{2,1,0:T(8,128)(2,1)} %bitcast.51), calls=%async_computation.7 | async-start | bytes 12582912 | tf_op jit(solution)/shard_map/all_to_all | solution.py:294
  680.6 644.7 %all-reduce.3.cloned.1.call-start = ((), (), s32[]{:S(2)}) async-start(), calls=%async_computation.8 | async-start | bytes 196608 | tf_op jit(solution)/shard_map/psum | solution.py:309
  688.0 201.0 %collective-permute-start.3 = (bf16[2048,1536]{1,0:T(8,128)(2,1)}, bf16[2048,1536]{1,0:T(8,128)(2,1)}, u32[]{:S(2)}, u32[]{:S(2)}) collective-permute-start(bf16[2048,1536]{1,0:T(8,128)(2,1)} %bitcast.5.rows_ref.own_ref), channel_id=1, source_target_pairs={{0,8},{8,0},{1,9},{9,1},{2,10},{10,2},{3,11},{11,3},{4,12},{12,4},... | collective-permute-start | bytes 18874376 | tf_op jit(solution)/shard_map/ppermute | solution.py:289
  690.3 289.3 %collective-permute-start.2 = (bf16[2048,1536]{1,0:T(8,128)(2,1)}, bf16[2048,1536]{1,0:T(8,128)(2,1)}, u32[]{:S(2)}, u32[]{:S(2)}) collective-permute-start(bf16[2048,1536]{1,0:T(8,128)(2,1)} %bitcast.11.rows_ref.own_ref), channel_id=1, source_target_pairs={{0,8},{8,0},{1,9},{9,1},{2,10},{10,2},{3,11},{11,3},{4,12},{12,4},... | collective-permute-start | bytes 18874376 | tf_op jit(solution)/shard_map/ppermute | solution.py:289
  690.4 407.2 %collective-permute-start.1 = (bf16[2048,1536]{1,0:T(8,128)(2,1)}, bf16[2048,1536]{1,0:T(8,128)(2,1)}, u32[]{:S(2)}, u32[]{:S(2)}) collective-permute-start(bf16[2048,1536]{1,0:T(8,128)(2,1)} %bitcast.15.rows_ref.own_ref), channel_id=1, source_target_pairs={{0,8},{8,0},{1,9},{9,1},{2,10},{10,2},{3,11},{11,3},{4,12},{12,4},... | collective-permute-start | bytes 18874376 | tf_op jit(solution)/shard_map/ppermute | solution.py:289
  692.3 539.6 %collective-permute-start = (bf16[2048,1536]{1,0:T(8,128)(2,1)}, bf16[2048,1536]{1,0:T(8,128)(2,1)}, u32[]{:S(2)}, u32[]{:S(2)}) collective-permute-start(bf16[2048,1536]{1,0:T(8,128)(2,1)} %bitcast.19.rows_ref.own_ref), channel_id=1, source_target_pairs={{0,8},{8,0},{1,9},{9,1},{2,10},{10,2},{3,11},{11,3},{4,12},{12,4},... | collective-permute-start | bytes 18874376 | tf_op jit(solution)/shard_map/ppermute | solution.py:289
  843.0 39.3 %slice-start = ((s8[12582912]{0:T(1024)(128)(4,1)}), s8[4194304]{0:T(1024)(128)(4,1)S(1)}, s32[]{:S(2)}) async-start(s8[12582912]{0:T(1024)(128)(4,1)} %bitcast.45), calls=%async_computation.9 | async-start | bytes 8388608
  843.0 39.2 %slice-start.1 = ((s8[12582912]{0:T(1024)(128)(4,1)}), s8[4194304]{0:T(1024)(128)(4,1)S(1)}, s32[]{:S(2)}) async-start(s8[12582912]{0:T(1024)(128)(4,1)} %bitcast.45), calls=%async_computation.10 | async-start | bytes 8388608
  856.6 25.7 %slice-start.2 = ((s8[12582912]{0:T(1024)(128)(4,1)}), s8[4194304]{0:T(1024)(128)(4,1)S(1)}, s32[]{:S(2)}) async-start(s8[12582912]{0:T(1024)(128)(4,1)} %bitcast.45), calls=%async_computation.11 | async-start | bytes 8388608
  1232.0 94.9 %copy-start.1 = (f32[768,32]{0,1:T(8,128)S(1)}, f32[768,32]{0,1:T(8,128)}, u32[]{:S(2)}) copy-start(f32[768,32]{0,1:T(8,128)} %param.12) | copy-start | bytes 294916
  (16 other events, 167.2 us)
Sparse Core Ops, SparseCore 0:
  889.1 64.9 all-reduce.2
